TPU v7x, 32 devices: a whole 2x2x4 slice. The times are simulated.
32 devices in a mesh: fsdp: 8 (over z, core), head: 4 (over y, x).
Axes of the slice: x: 2, y: 2, z: 4, core: 2. Of those that a mesh axis runs over, the one named last changes fastest.
Arguments:
- probe_compressed: bfloat16 [2, 32, 1536], P(None, 'fsdp'), may hold values from -6 to 6
- w_uq: bfloat16 [1536, 16384], P('fsdp', 'head'), may hold values from -0.15625 to 0.15625
- w_qr: bfloat16 [1536, 8192], P('fsdp', 'head'), may hold values from -0.15625 to 0.15625
- w_uk: bfloat16 [512, 16384], P('fsdp', 'head'), may hold values from -0.25 to 0.25
- w_uv: bfloat16 [512, 16384], P('fsdp', 'head'), may hold values from -1.5 to 1.5
- cache: bfloat16 [32, 1024, 576], P(('fsdp', 'head')), may hold values from -136 to 136
- new_kv: bfloat16 [2, 32, 576], P(None, ('fsdp', 'head')), may hold values from -6 to 6
- lengths: int32 [32], P(('fsdp', 'head')), may hold values from 1 to 1024
Outputs:
- values: bfloat16 [2, 32, 16384], P(None, 'fsdp', 'head')
All inputs are finite; a program needn't handle non-finite values.
Results may differ from a plain program's by a relative error of at most 0.035.
Values may be sent and summed in bfloat16 or wider, within the bound.
A program may use at most 64 MiB of HBM per device.

v0:
```python
import functools

import jax
import jax.numpy as jnp
import numpy as np
from jax import lax
from jax.experimental import pallas as pl
from jax.experimental.pallas import tpu as pltpu
from jax.sharding import PartitionSpec as P

NOPE = 128
R = 64
VDIM = 128


def rotate(rope_part, position):
    half = rope_part.shape[-1] // 2
    freqs = 10000.0 ** (-(jnp.arange(half, dtype=jnp.float32) * 2.0 / (2 * half)))
    angle = position[..., None] * freqs
    first = rope_part[..., :half]
    second = rope_part[..., half:]
    cosine_table = jnp.cos(angle)
    sine = jnp.sin(angle)
    return jnp.concatenate(
        [first * cosine_table - second * sine, first * sine + second * cosine_table], axis=-1
    )


def attend(query, keys, fresh, extent):
    steps = query.shape[0]
    heads = query.shape[1]
    width = keys.shape[1]
    latent_width = width - R
    position = (extent + jnp.arange(steps, dtype=jnp.int32)).astype(jnp.float32)
    rotated = rotate(query[:, :, latent_width:].astype(jnp.float32), position[:, None])
    joined = jnp.concatenate([query[:, :, :latent_width], rotated.astype(jnp.bfloat16)], axis=2)
    joined = joined.reshape(steps * heads, width)
    factor = (NOPE + R) ** (-0.5)
    older = jnp.dot(joined, keys.T, preferred_element_type=jnp.float32) * factor
    valid = jnp.arange(keys.shape[0], dtype=jnp.int32) < extent
    older = jnp.where(valid[None, :], older, -1e30)
    newer = jnp.dot(joined, fresh.T, preferred_element_type=jnp.float32) * factor
    order = jnp.arange(steps, dtype=jnp.int32)
    allowed = jnp.repeat(order[None, :] <= order[:, None], heads, axis=0)
    newer = jnp.where(allowed, newer, -1e30)
    highest = jnp.maximum(jnp.max(older, axis=1), jnp.max(newer, axis=1))
    weight_old = jnp.exp(older - highest[:, None])
    weight_new = jnp.exp(newer - highest[:, None])
    total = jnp.sum(weight_old, axis=1) + jnp.sum(weight_new, axis=1)
    mixed = jnp.dot(
        weight_old.astype(jnp.bfloat16), keys[:, :latent_width], preferred_element_type=jnp.float32
    )
    mixed = mixed + jnp.dot(
        weight_new.astype(jnp.bfloat16), fresh[:, :latent_width], preferred_element_type=jnp.float32
    )
    return (mixed / total[:, None]).astype(jnp.bfloat16).reshape(steps, heads, latent_width)


def per_device(probe_compressed, w_uq, w_qr, w_uk, w_uv, cache, new_kv, lengths):
    heads = w_uk.shape[1] // NOPE
    steps, group, rank = probe_compressed.shape
    flattened = probe_compressed.reshape(steps * group, rank)
    key_up, value_up, rotary_up_weight = (
        lax.all_gather(w_uk, "fsdp", axis=0, tiled=True),
        lax.all_gather(w_uv, "fsdp", axis=0, tiled=True),
        lax.all_gather(w_qr, "fsdp", axis=0, tiled=True),
    )
    key_heads = key_up.reshape(key_up.shape[0], heads, NOPE)
    slab = lax.all_gather(w_uq, "fsdp", axis=0, tiled=True)
    count = slab.shape[0]
    slab_heads = slab.reshape(count, heads, NOPE)
    absorbed = jnp.einsum("rhn,chn->hrc", slab_heads, key_heads, preferred_element_type=jnp.float32)
    absorbed = absorbed.astype(jnp.bfloat16)
    summed = jnp.einsum("qr,hrc->qhc", flattened, absorbed, preferred_element_type=jnp.float32)
    latent = summed.astype(jnp.bfloat16)
    latent_rank = key_up.shape[0]
    rope_query = jnp.dot(flattened, rotary_up_weight, preferred_element_type=jnp.float32).astype(
        jnp.bfloat16
    )
    rope_query = rope_query.reshape(steps * group, heads, R)
    query_matrix = jnp.concatenate([latent, rope_query], axis=2).reshape(
        steps, group, heads, latent_rank + R
    )
    row_queries = lax.all_to_all(query_matrix, "head", split_axis=1, concat_axis=2, tiled=True)
    mixed = jax.vmap(attend, in_axes=(1, 0, 1, 0), out_axes=1)(row_queries, cache, new_kv, lengths)
    combined_across_heads = lax.all_to_all(mixed, "head", split_axis=2, concat_axis=1, tiled=True)
    value_heads = value_up.reshape(latent_rank, heads, VDIM)
    attention_output = jnp.einsum(
        "sghc,chv->sghv", combined_across_heads, value_heads, preferred_element_type=jnp.float32
    )
    return attention_output.astype(jnp.bfloat16).reshape(steps, group, heads * VDIM)


def fused(F, G, steps, own,
          len_ref, freq_hbm, probe_hbm, new_hbm, uq_hbm, qr_hbm, uk_hbm, uv_hbm, cache_hbm,
          out_ref,
          freq_ref, probe_ref, new_ref,
          uq, wqr, wk, wv, kv, ps, pr, pp, pv, zs, zr, nq, es_, er_, qs, qr, ms, mr, vs, vr,
          lsem, sp, rp, sk, rk, spp, rpp, sz, rz, sn, rn, se, re_, sq, rq, sm, rm, so, ro):
    f32, bf16 = jnp.float32, jnp.bfloat16
    f = lax.axis_index("fsdp")
    hd = lax.axis_index("head")
    N = F * G
    Z = F // 2
    me = f * G + hd
    z, core = lax.div(f, 2), lax.rem(f, 2)
    ck = uk_hbm.shape[0]
    cols = own * NOPE
    rcols = own * R
    C = ck * F
    stored = cache_hbm.shape[2]
    slice_rank = uq.shape[0]
    per = steps * own
    queries = F * steps * G
    expanded = N * per

    def rcopy(src, dst, ssem, rsem, ff, hh):
        return pltpu.make_async_remote_copy(
            src_ref=src, dst_ref=dst, send_sem=ssem, recv_sem=rsem,
            device_id={"fsdp": ff, "head": hh}, device_id_type=pl.DeviceIdType.MESH,
        )

    def block(t, width):
        return pl.ds(pl.multiple_of(t * width, 128), width)

    hcols = Z * cols
    mine = pl.ds(pl.multiple_of(core * ck, 16), ck)
    load_uq = pltpu.make_async_copy(uq_hbm, uq, lsem.at[0])
    load_qr = pltpu.make_async_copy(qr_hbm, wqr, lsem.at[1])
    load_kv = pltpu.make_async_copy(cache_hbm.at[0], kv, lsem.at[2])
    load_uk = pltpu.make_async_copy(uk_hbm.at[:, block(core, hcols)], wk.at[mine], lsem.at[3])
    load_uv = pltpu.make_async_copy(uv_hbm.at[:, block(core, hcols)], wv.at[mine], lsem.at[4])
    load_probe = pltpu.make_async_copy(probe_hbm, probe_ref, lsem.at[5])
    load_new = pltpu.make_async_copy(new_hbm, new_ref, lsem.at[6])
    load_freq = pltpu.make_async_copy(freq_hbm, freq_ref, lsem.at[7])
    loads = [load_probe, load_uq, load_qr, load_new, load_freq, load_uk, load_kv, load_uv]
    for c in loads:
        c.start()

    bar = pltpu.get_barrier_semaphore()

    def greet(k, carry):
        t = lax.rem(me + k, N)
        pl.semaphore_signal(
            bar, inc=1, device_id={"fsdp": lax.div(t, G), "head": lax.rem(t, G)},
            device_id_type=pl.DeviceIdType.MESH,
        )
        return carry

    lax.fori_loop(1, N, greet, 0)

    load_probe.wait()
    probe8 = jnp.concatenate([probe_ref[s].astype(f32) for s in range(steps)], axis=0)
    for p in range(F):
        ps[p] = probe8[:, p * slice_rank:(p + 1) * slice_rank].astype(bf16)
    pr[pl.ds(f, 1)] = ps[pl.ds(f, 1)]

    pl.semaphore_wait(bar, N - 1)

    def probe_copy(k):
        t = lax.rem(f + k, F)
        return rcopy(ps.at[t], pr.at[f], sp.at[k], rp.at[f], t, hd)

    def weight_copy(i):
        hbm, w = ((uk_hbm, wk), (uv_hbm, wv))[i]
        return rcopy(hbm.at[:, block(1 - core, hcols)], w.at[mine], sk.at[i], rk.at[i], z * 2 + 1 - core, hd)

    def each(first, last, make, method):
        def step(k, carry):
            getattr(make(k), method)()
            return carry
        lax.fori_loop(first, last, step, 0)

    each(1, F, probe_copy, "start")
    weight_copy(0).start()
    weight_copy(1).start()

    load_new.wait()
    load_freq.wait()
    at = lax.broadcasted_iota(jnp.int32, (128, C + R), 0)
    fill = jnp.zeros((128, C + R), f32)
    for s in range(steps):
        fill = jnp.where(at == s, new_ref[0, s:s + 1].astype(f32), fill)
    fresh = fill.astype(bf16)

    row8 = lax.broadcasted_iota(jnp.int32, (per, 128), 0)
    step8 = lax.div(row8, own)
    angle = (len_ref[0] + step8).astype(f32) * freq_ref[...]
    cos8, sin8 = jnp.cos(angle), jnp.sin(angle)

    load_uq.wait()
    load_qr.wait()

    def probe_arrival(k, carry):
        src = lax.rem(f + k, F)
        rcopy(ps.at[src], pr.at[src], sp.at[k], rp.at[src], src, hd).wait_recv()
        return carry

    lax.fori_loop(1, F, probe_arrival, 0)
    probes = pr[...].astype(f32).reshape(queries, slice_rank).astype(bf16)

    def partial_of(t):
        a = jnp.dot(probes, uq[:, block(t, cols)], preferred_element_type=f32)
        b = jnp.dot(probes, wqr[:, block(t, rcols)], preferred_element_type=f32)
        return a, b

    def pair_copy(k):
        zz = lax.rem(z + k, Z)
        return rcopy(pp.at[zz], pv.at[zz], spp.at[zz], rpp.at[zz], z * 2 + 1 - core, hd)

    def to_partner(k, carry):
        zz = lax.rem(z + k, Z)
        a, b = partial_of((1 - core) * Z + zz)
        pp[zz, :, 0:cols] = a.astype(bf16)
        pp[zz, :, cols:cols + rcols] = b.astype(bf16)
        pair_copy(k).start()
        return carry

    lax.fori_loop(1, Z + 1, to_partner, 0)

    def line_copy(k):
        zz = lax.rem(z + k, Z)
        return rcopy(zs.at[zz], zr.at[z], sz.at[zz], rz.at[z], zz * 2 + core, hd)

    def along_line(k, carry):
        zz = lax.rem(z + k, Z)
        a, b = partial_of(core * Z + zz)
        pair_copy(k).wait_recv()
        zs[zz, :, 0:cols] = (a + pv[zz, :, 0:cols].astype(f32)).astype(bf16)
        zs[zz, :, cols:cols + rcols] = (b + pv[zz, :, cols:cols + rcols].astype(f32)).astype(bf16)
        line_copy(k).start()
        return carry

    lax.fori_loop(1, Z, along_line, 0)
    a, b = partial_of(core * Z + z)
    pair_copy(0).wait_recv()
    nope = a + pv[z, :, 0:cols].astype(f32)
    rope = b + pv[z, :, cols:cols + rcols].astype(f32)
    for k in range(1, Z):
        src = lax.rem(z + k, Z)
        rcopy(zs.at[src], zr.at[src], sz.at[src], rz.at[src], src * 2 + core, hd).wait_recv()
        nope = nope + zr[src, :, 0:cols].astype(f32)
        rope = rope + zr[src, :, cols:cols + rcols].astype(f32)
    nq[pl.ds(z, 1)] = nope.astype(bf16).reshape(1, queries, cols)
    rope = rope.astype(bf16)

    def nope_copy(k):
        zz = lax.rem(z + k, Z)
        return rcopy(nq.at[z], nq.at[z], sn.at[k], rn.at[z], zz * 2 + core, hd)

    each(1, Z, nope_copy, "start")

    def iota(shape, axis):
        return lax.broadcasted_iota(jnp.int32, shape, axis)

    er = iota((expanded, queries), 0)
    ed = lax.div(er, per)
    es = lax.div(lax.rem(er, per), own)
    pick = (lax.div(ed, G) * (steps * G) + es * G + lax.rem(ed, G)) == iota((expanded, queries), 1)
    pick = jnp.where(pick, 1.0, 0.0).astype(bf16)
    head_of_row = lax.rem(iota((expanded, cols), 0), own)
    own_head = lax.div(iota((expanded, cols), 1), NOPE) == head_of_row
    own_rope = lax.div(iota((expanded, rcols), 1), R) == lax.rem(iota((expanded, rcols), 0), own)
    fold = lax.rem(iota((rcols, 128), 0), R) == iota((rcols, 128), 1)
    fold = jnp.where(fold, 1.0, 0.0).astype(bf16)
    wide_rope = jnp.where(own_rope, jnp.dot(pick, rope, preferred_element_type=f32), 0.0).astype(bf16)
    rope_rows = jnp.dot(wide_rope, fold, preferred_element_type=f32)
    es_[...] = rope_rows.reshape(N, per, 128).astype(bf16)
    part = hd * 2 + core
    slot = part * Z + z

    def rope_copy(k):
        t = lax.rem(me + k, N)
        return rcopy(es_.at[t], er_.at[slot], se.at[k], re_.at[slot], lax.div(t, G), lax.rem(t, G))

    each(1, N, rope_copy, "start")
    er_[pl.ds(slot, 1)] = es_[pl.ds(me, 1)]

    load_uk.wait()
    theirs = pl.ds(pl.multiple_of((1 - core) * ck, 16), ck)

    def weight_arrival(i):
        hbm, w = ((uk_hbm, wk), (uv_hbm, wv))[i]
        rcopy(hbm.at[:, block(core, hcols)], w.at[theirs], sk.at[i], rk.at[i], z * 2 + 1 - core, hd).wait_recv()

    weight_arrival(0)
    for k in range(1, Z):
        src = lax.rem(z + k, Z)
        rcopy(nq.at[src], nq.at[src], sn.at[k], rn.at[src], src * 2 + core, hd).wait_recv()
    for h in range(Z):
        wide = jnp.where(own_head, jnp.dot(pick, nq[h], preferred_element_type=f32), 0.0).astype(bf16)
        latent = lax.dot_general(
            wide, wk[:, h * cols:(h + 1) * cols], (((1,), (1,)), ((), ())), preferred_element_type=f32
        )
        qs[:, h * per:(h + 1) * per, :] = latent.reshape(N, per, 2 * ck).astype(bf16)

    tall = Z * per

    def tile(p, zz):
        return (pl.ds(pl.multiple_of(p * tall, 16), tall), pl.ds(pl.multiple_of(zz * 2 * ck, 128), 2 * ck))

    def query_copy(k):
        ff = lax.rem(f + lax.rem(k, F), F)
        hh = lax.rem(hd + lax.div(k, F), G)
        return rcopy(qs.at[ff * G + hh], qr.at[tile(part, z)], sq.at[k], rq.at[slot], ff, hh)

    each(1, N, query_copy, "start")
    qr[tile(part, z)] = qs[pl.ds(me, 1)].reshape(tall, 2 * ck)

    load_kv.wait()
    factor = (NOPE + R) ** -0.5
    chunk = F
    keys = stored + 128
    sr = iota((128, 128), 0)
    sc = iota((128, 128), 1)
    half = R // 2
    swap = jnp.where((sr == sc + half) & (sc < half), -1.0, 0.0)
    swap = swap + jnp.where((sr == sc - half) & (sc >= half) & (sc < R), 1.0, 0.0)
    swap = swap.astype(bf16)
    rows = chunk * per
    cosines = jnp.broadcast_to(cos8[None], (chunk, per, 128)).reshape(rows, 128)
    sines = jnp.broadcast_to(sin8[None], (chunk, per, 128)).reshape(rows, 128)
    column = iota((rows, keys), 1)
    step_of = lax.div(lax.rem(iota((rows, keys), 0), per), own)
    shown = (column < len_ref[0]) | ((column >= stored) & (column <= stored + step_of))

    def mixed_copy(b, i):
        zz, cc = lax.div(i, 2), lax.rem(i, 2)
        e = i * G + b
        return rcopy(ms.at[tile(b * 2 + cc, zz)], mr.at[me], sm.at[e], rm.at[me], i, b)

    def attend_chunk(turn, carry):
        b = lax.rem(hd + G - turn, G)

        def arrival(i, c):
            zz, cc = lax.div(i, 2), lax.rem(i, 2)
            at_slot = (b * 2 + cc) * Z + zz

            @pl.when(i * G + b != me)
            def _():
                rcopy(es_.at[0], er_.at[at_slot], se.at[0], re_.at[at_slot], i, b).wait_recv()
                rcopy(qs.at[0], qr.at[tile(b * 2 + cc, zz)], sq.at[0], rq.at[at_slot], i, b).wait_recv()
            return c

        lax.fori_loop(0, chunk, arrival, 0)
        here = pl.ds(pl.multiple_of(b * rows, 16), rows)
        lat = qr[here, :]
        xr = er_[pl.ds(b * chunk, chunk)].astype(f32).reshape(rows, 128)
        turned = jnp.dot(xr.astype(bf16), swap, preferred_element_type=f32)
        rot = (xr * cosines + turned * sines).astype(bf16)[:, 0:R]
        nt = (((1,), (1,)), ((), ()))
        s = jnp.dot(lat, kv[0:C, :], preferred_element_type=f32)
        s = s + jnp.dot(rot, kv[C:C + R, :], preferred_element_type=f32)
        n = lax.dot_general(lat, fresh[:, 0:C], nt, preferred_element_type=f32)
        n = n + lax.dot_general(rot, fresh[:, C:C + R], nt, preferred_element_type=f32)
        s = jnp.concatenate([s, n], axis=1)
        s = jnp.where(shown, s * factor, -1e30)
        m = jnp.max(s, axis=1, keepdims=True)
        w = jnp.exp(s - m)
        total = jnp.sum(w, axis=1, keepdims=True)
        w = w.astype(bf16)
        mix = lax.dot_general(w[:, 0:stored], kv[0:C, :], nt, preferred_element_type=f32)
        mix = mix + jnp.dot(w[:, stored:], fresh[:, 0:C], preferred_element_type=f32)
        ms[here, :] = (mix / total).astype(bf16)

        def send(i, c):
            @pl.when(i * G + b != me)
            def _():
                mixed_copy(b, i).start()
            return c

        lax.fori_loop(0, chunk, send, 0)
        return carry

    lax.fori_loop(0, G, attend_chunk, 0)
    mr[pl.ds(me, 1)] = ms[tile(part, z)].reshape(1, tall, 2 * ck)

    load_uv.wait()
    weight_arrival(1)

    def mixed_arrival(k, carry):
        src = lax.rem(me + k, N)
        rcopy(ms.at[tile(0, 0)], mr.at[src], sm.at[src], rm.at[src], lax.div(src, G), lax.rem(src, G)).wait_recv()
        return carry

    lax.fori_loop(1, N, mixed_arrival, 0)
    for h in range(Z):
        mixed = mr[:, h * per:(h + 1) * per, :].astype(f32).reshape(expanded, 2 * ck).astype(bf16)
        values = jnp.dot(mixed, wv[:, h * cols:(h + 1) * cols], preferred_element_type=f32)
        values = jnp.where(own_head, values, 0.0).astype(bf16)
        values = lax.dot_general(pick, values, (((0,), (0,)), ((), ())), preferred_element_type=f32)
        vs[:, :, h * cols:(h + 1) * cols] = values.reshape(F, steps * G, cols).astype(bf16)

    def out_copy(k):
        t = lax.rem(f + k, F)
        return rcopy(vs.at[t], vr.at[f], so.at[k], ro.at[f], t, hd)

    each(1, F, out_copy, "start")
    vr[pl.ds(f, 1)] = vs[pl.ds(f, 1)]

    def out_arrival(k, carry):
        src = lax.rem(f + k, F)
        rcopy(vs.at[src], vr.at[src], so.at[k], ro.at[src], src, hd).wait_recv()
        return carry

    lax.fori_loop(1, F, out_arrival, 0)
    for p in range(2):
        v = sum(vr[zz * 2 + p].astype(f32) for zz in range(Z))
        for s in range(steps):
            out_ref[s, :, p * hcols:(p + 1) * hcols] = v[s * G:(s + 1) * G].astype(bf16)

    each(1, F, probe_copy, "wait_send")
    weight_copy(0).wait_send()
    weight_copy(1).wait_send()
    each(1, Z, nope_copy, "wait_send")
    each(1, N, rope_copy, "wait_send")
    each(1, Z + 1, pair_copy, "wait_send")
    each(1, Z, line_copy, "wait_send")
    each(1, N, query_copy, "wait_send")
    each(1, F, out_copy, "wait_send")

    def mixed_sent(k, carry):
        t = lax.rem(me + k, N)
        mixed_copy(lax.rem(t, G), lax.div(t, G)).wait_send()
        return carry

    lax.fori_loop(1, N, mixed_sent, 0)


def one_kernel(probe_compressed, w_uq, w_qr, w_uk, w_uv, cache, new_kv, lengths):
    F, G = lax.axis_size("fsdp"), lax.axis_size("head")
    N, Z = F * G, F // 2
    steps, group, _ = probe_compressed.shape
    ck, heads = w_uk.shape[0], w_uk.shape[1] // NOPE
    own = heads // F
    C = ck * F
    queries = F * steps * G
    per = steps * own
    cols, rcols = own * NOPE, own * R
    hcols = Z * cols
    cache = cache.transpose(0, 2, 1)
    new_kv = new_kv.transpose(1, 0, 2)
    half = R // 2
    freqs = 10000.0 ** (-(np.arange(half, dtype=np.float32) * 2.0 / R))
    freqs = np.concatenate([freqs, freqs, np.zeros(128 - R)]).astype(np.float32)[None]
    bf16 = jnp.bfloat16
    vm = lambda *shape: pltpu.VMEM(shape, bf16)
    dma = lambda n: pltpu.SemaphoreType.DMA((n,))
    vmem = pl.BlockSpec(memory_space=pltpu.VMEM)
    hbm = pl.BlockSpec(memory_space=pltpu.HBM)
    return pl.pallas_call(
        functools.partial(fused, F, G, steps, own),
        out_shape=jax.ShapeDtypeStruct((steps, group, heads * VDIM), bf16),
        in_specs=[pl.BlockSpec(memory_space=pltpu.SMEM)] + [hbm] * 8,
        out_specs=vmem,
        scratch_shapes=[
            pltpu.VMEM((1, 128), jnp.float32), vm(*probe_compressed.shape), vm(*new_kv.shape),
            vm(*w_uq.shape), vm(*w_qr.shape), vm(2 * ck, hcols), vm(2 * ck, hcols), vm(*cache.shape[1:]),
            vm(F, steps * G, w_uq.shape[0]), vm(F, steps * G, w_uq.shape[0]),
            vm(Z, queries, cols + rcols), vm(Z, queries, cols + rcols),
            vm(Z, queries, cols + rcols), vm(Z, queries, cols + rcols),
            vm(Z, queries, cols), vm(N, per, 128), vm(N, per, 128),
            vm(N, Z * per, 2 * ck), vm(2 * G * Z * per, C), vm(2 * G * Z * per, C), vm(N, Z * per, 2 * ck),
            vm(F, steps * G, hcols), vm(F, steps * G, hcols),
            dma(8), dma(F), dma(F), dma(2), dma(2), dma(Z), dma(Z), dma(Z), dma(Z), dma(Z), dma(Z),
            dma(N), dma(N), dma(N), dma(N), dma(N), dma(N), dma(F), dma(F),
        ],
        compiler_params=pltpu.CompilerParams(
            collective_id=0, has_side_effects=True, vmem_limit_bytes=67043328
        ),
    )(lengths, jnp.asarray(freqs), probe_compressed, new_kv, w_uq, w_qr, w_uk, w_uv, cache)


def choose(*arrays):
    probe, w_uk, cache = arrays[0], arrays[3], arrays[5]
    F, G = lax.axis_size("fsdp"), lax.axis_size("head")
    own = w_uk.shape[1] // NOPE // F
    fits = own > 0 and w_uk.shape[1] == own * NOPE * F and F % 2 == 0
    fits = fits and probe.shape[1] == G and cache.shape[0] == 1
    fits = fits and (probe.shape[0] * own) % 8 == 0 and (probe.shape[0] * G) % 8 == 0
    fits = fits and w_uk.shape[0] % 16 == 0 and (2 * w_uk.shape[0]) % 128 == 0 and cache.shape[1] % 128 == 0 and (own * R) % 128 == 0
    return one_kernel(*arrays) if fits else per_device(*arrays)


def solution(mesh):
    in_specs = (
        P(None, "fsdp", None),
        P("fsdp", "head"),
        P("fsdp", "head"),
        P("fsdp", "head"),
        P("fsdp", "head"),
        P(("fsdp", "head"), None, None),
        P(None, ("fsdp", "head"), None),
        P(("fsdp", "head")),
    )
    out_specs = P(None, "fsdp", "head")
    return jax.shard_map(
        choose, mesh=mesh, in_specs=in_specs, out_specs=out_specs, check_vma=False
    )
```

profile of v0, /device:TPU:1, one launch (start us, length us, event | category | flops | bytes accessed | tf_op | source)
XLA Modules:
  0.0 57.9 jit_solution(12828568503306557645)
XLA Ops:
  0.7 55.7 %shard_map.91 = bf16[2,4,4096]{2,1,0:T(4,128)(2,1)} custom-call(s32[1]{0:T(128)S(6)} %copy.11.len_ref, f32[1,128]{1,0:T(1,128)} %constant.2.clone.freq_hbm, bf16[2,4,1536]{2,1,0:T(4,128)(2,1)} %probe_hbm.1, bf16[1,2,576]{2,1,0:T(2,128)(2,1)} %bitcast.3, bf16[192,4096]{1,0:T(8,128)(2,1)} %uq_hbm.1, bf16[192,2048]{1,0:T(8,128)(2,1)} %qr_hbm.1, ...), custom_call_target="tpu_custom_call" | custom-call | tf_op jit(solution)/shard_map/pallas_call | solution.py:451
  56.4 1.5 %copy.12 = bf16[2,4,4096]{2,1,0:T(4,128)(2,1)} copy(bf16[2,4,4096]{2,1,0:T(4,128)(2,1)} %shard_map.91) | data formatting | bytes 131072
where the time goes:
time: 58.1 us; the launch traced here: 57.9 us
  Pallas kernels  55.7 us (96%)
  local copies, waits for them, and re-layouts  1.49 us (3%)
  between operations  0.66 us (1%)
    pallas_call x1, Pallas kernels, one_kernel(): pl.pallas_call(functools.partial(fused, F, G, steps, own), out_shape=jax....  55.7 us
    unnamed x1, local copies, waits for them, and re-layouts  1.49 us

commit v1 on v0

v1 whole, which is shorter than its diff:
```python
import functools

import jax
import jax.numpy as jnp
import numpy as np
from jax import lax
from jax.experimental import pallas as pl
from jax.experimental.pallas import tpu as pltpu
from jax.sharding import PartitionSpec as P

NOPE = 128
R = 64
VDIM = 128


def rotate(rope_part, position):
    half = rope_part.shape[-1] // 2
    freqs = 10000.0 ** (-(jnp.arange(half, dtype=jnp.float32) * 2.0 / (2 * half)))
    angle = position[..., None] * freqs
    first = rope_part[..., :half]
    second = rope_part[..., half:]
    cosine_table = jnp.cos(angle)
    sine = jnp.sin(angle)
    return jnp.concatenate(
        [first * cosine_table - second * sine, first * sine + second * cosine_table], axis=-1
    )


def attend(query, keys, fresh, extent):
    steps = query.shape[0]
    heads = query.shape[1]
    width = keys.shape[1]
    latent_width = width - R
    position = (extent + jnp.arange(steps, dtype=jnp.int32)).astype(jnp.float32)
    rotated = rotate(query[:, :, latent_width:].astype(jnp.float32), position[:, None])
    joined = jnp.concatenate([query[:, :, :latent_width], rotated.astype(jnp.bfloat16)], axis=2)
    joined = joined.reshape(steps * heads, width)
    factor = (NOPE + R) ** (-0.5)
    older = jnp.dot(joined, keys.T, preferred_element_type=jnp.float32) * factor
    valid = jnp.arange(keys.shape[0], dtype=jnp.int32) < extent
    older = jnp.where(valid[None, :], older, -1e30)
    newer = jnp.dot(joined, fresh.T, preferred_element_type=jnp.float32) * factor
    order = jnp.arange(steps, dtype=jnp.int32)
    allowed = jnp.repeat(order[None, :] <= order[:, None], heads, axis=0)
    newer = jnp.where(allowed, newer, -1e30)
    highest = jnp.maximum(jnp.max(older, axis=1), jnp.max(newer, axis=1))
    weight_old = jnp.exp(older - highest[:, None])
    weight_new = jnp.exp(newer - highest[:, None])
    total = jnp.sum(weight_old, axis=1) + jnp.sum(weight_new, axis=1)
    mixed = jnp.dot(
        weight_old.astype(jnp.bfloat16), keys[:, :latent_width], preferred_element_type=jnp.float32
    )
    mixed = mixed + jnp.dot(
        weight_new.astype(jnp.bfloat16), fresh[:, :latent_width], preferred_element_type=jnp.float32
    )
    return (mixed / total[:, None]).astype(jnp.bfloat16).reshape(steps, heads, latent_width)


def per_device(probe_compressed, w_uq, w_qr, w_uk, w_uv, cache, new_kv, lengths):
    heads = w_uk.shape[1] // NOPE
    steps, group, rank = probe_compressed.shape
    flattened = probe_compressed.reshape(steps * group, rank)
    key_up, value_up, rotary_up_weight = (
        lax.all_gather(w_uk, "fsdp", axis=0, tiled=True),
        lax.all_gather(w_uv, "fsdp", axis=0, tiled=True),
        lax.all_gather(w_qr, "fsdp", axis=0, tiled=True),
    )
    key_heads = key_up.reshape(key_up.shape[0], heads, NOPE)
    slab = lax.all_gather(w_uq, "fsdp", axis=0, tiled=True)
    count = slab.shape[0]
    slab_heads = slab.reshape(count, heads, NOPE)
    absorbed = jnp.einsum("rhn,chn->hrc", slab_heads, key_heads, preferred_element_type=jnp.float32)
    absorbed = absorbed.astype(jnp.bfloat16)
    summed = jnp.einsum("qr,hrc->qhc", flattened, absorbed, preferred_element_type=jnp.float32)
    latent = summed.astype(jnp.bfloat16)
    latent_rank = key_up.shape[0]
    rope_query = jnp.dot(flattened, rotary_up_weight, preferred_element_type=jnp.float32).astype(
        jnp.bfloat16
    )
    rope_query = rope_query.reshape(steps * group, heads, R)
    query_matrix = jnp.concatenate([latent, rope_query], axis=2).reshape(
        steps, group, heads, latent_rank + R
    )
    row_queries = lax.all_to_all(query_matrix, "head", split_axis=1, concat_axis=2, tiled=True)
    mixed = jax.vmap(attend, in_axes=(1, 0, 1, 0), out_axes=1)(row_queries, cache, new_kv, lengths)
    combined_across_heads = lax.all_to_all(mixed, "head", split_axis=2, concat_axis=1, tiled=True)
    value_heads = value_up.reshape(latent_rank, heads, VDIM)
    attention_output = jnp.einsum(
        "sghc,chv->sghv", combined_across_heads, value_heads, preferred_element_type=jnp.float32
    )
    return attention_output.astype(jnp.bfloat16).reshape(steps, group, heads * VDIM)


def fused(F, G, steps, own,
          len_ref, freq_hbm, probe_hbm, new_hbm, uq_hbm, qr_hbm, uk_hbm, uv_hbm, cache_hbm,
          out_ref,
          freq_ref, probe_ref, new_ref,
          uq, wqr, wk, wv, kv, ps, pr, pp, pv, ppr, pvr, ls, lr, lsr, lrr, hs, hr, hsr, hrr,
          es_, er_, qs, qr, ms, mr, vs, vr,
          lsem, sp, rp, sk, rk, spp, rpp, sppr, rppr, sl, rl, slr, rlr, sh, rh, shr, rhr,
          se, re_, sq, rq, sm, rm, so, ro):
    f32, bf16 = jnp.float32, jnp.bfloat16
    f = lax.axis_index("fsdp")
    hd = lax.axis_index("head")
    N = F * G
    U = F // 4
    me = f * G + hd
    u, v, core = lax.div(f, 4), lax.rem(lax.div(f, 2), 2), lax.rem(f, 2)
    quad = lax.rem(f, 4)
    part = core * 2 + v
    ck = uk_hbm.shape[0]
    cols = own * NOPE
    rcols = own * R
    bcols, brcols = U * cols, U * rcols
    C = ck * F
    wide_c = 4 * ck
    stored = cache_hbm.shape[2]
    slice_rank = uq.shape[0]
    per = steps * own
    tall = U * per
    queries = F * steps * G
    half_queries = queries // U
    expanded = N * per

    def rcopy(src, dst, ssem, rsem, ff, hh):
        return pltpu.make_async_remote_copy(
            src_ref=src, dst_ref=dst, send_sem=ssem, recv_sem=rsem,
            device_id={"fsdp": ff, "head": hh}, device_id_type=pl.DeviceIdType.MESH,
        )

    def block(t, width):
        return pl.ds(pl.multiple_of(t * width, 128), width)

    def each(first, last, make, method):
        def step(k, carry):
            getattr(make(k), method)()
            return carry
        lax.fori_loop(first, last, step, 0)

    def iota(shape, axis):
        return lax.broadcasted_iota(jnp.int32, shape, axis)

    mine = pl.ds(pl.multiple_of(quad * ck, 16), ck)
    load_uq = pltpu.make_async_copy(uq_hbm, uq, lsem.at[0])
    load_qr = pltpu.make_async_copy(qr_hbm, wqr, lsem.at[1])
    load_kv = pltpu.make_async_copy(cache_hbm.at[0], kv, lsem.at[2])
    load_uk = pltpu.make_async_copy(uk_hbm.at[:, block(part, bcols)], wk.at[mine], lsem.at[3])
    load_uv = pltpu.make_async_copy(uv_hbm.at[:, block(part, bcols)], wv.at[mine], lsem.at[4])
    load_probe = pltpu.make_async_copy(probe_hbm, probe_ref, lsem.at[5])
    load_new = pltpu.make_async_copy(new_hbm, new_ref, lsem.at[6])
    load_freq = pltpu.make_async_copy(freq_hbm, freq_ref, lsem.at[7])
    loads = [load_probe, load_uq, load_qr, load_new, load_freq, load_uk, load_kv, load_uv]
    for c in loads:
        c.start()

    bar = pltpu.get_barrier_semaphore()

    def greet(k, carry):
        t = lax.rem(me + k, N)
        pl.semaphore_signal(
            bar, inc=1, device_id={"fsdp": lax.div(t, G), "head": lax.rem(t, G)},
            device_id_type=pl.DeviceIdType.MESH,
        )
        return carry

    lax.fori_loop(1, N, greet, 0)

    load_probe.wait()
    probe8 = jnp.concatenate([probe_ref[s].astype(f32) for s in range(steps)], axis=0)
    for p in range(F):
        ps[p] = probe8[:, p * slice_rank:(p + 1) * slice_rank].astype(bf16)
    pr[pl.ds(f, 1)] = ps[pl.ds(f, 1)]

    pl.semaphore_wait(bar, N - 1)

    def probe_copy(k):
        t = lax.rem(f + k, F)
        return rcopy(ps.at[t], pr.at[f], sp.at[0], rp.at[0], t, hd)

    def weight_copy(i, k):
        hbm, w = ((uk_hbm, wk), (uv_hbm, wv))[i]
        t = lax.rem(quad + k, 4)
        there = lax.rem(t, 2) * 2 + lax.div(t, 2)
        return rcopy(hbm.at[:, block(there, bcols)], w.at[mine], sk.at[i], rk.at[i], u * 4 + t, hd)

    def weight_wait(i, method):
        w = (wk, wv)[i].at[pl.ds(0, 3 * ck)]
        getattr(rcopy(w, w, sk.at[i], rk.at[i], f, hd), method)()

    each(1, F, probe_copy, "start")
    each(1, 4, functools.partial(weight_copy, 0), "start")

    load_new.wait()
    load_freq.wait()
    at = iota((128, C + R), 0)
    fill = jnp.zeros((128, C + R), f32)
    for s in range(steps):
        fill = jnp.where(at == s, new_ref[0, s:s + 1].astype(f32), fill)
    fresh = fill.astype(bf16)

    step8 = lax.div(iota((per, 128), 0), own)
    angle = (len_ref[0] + step8).astype(f32) * freq_ref[...]
    cos8, sin8 = jnp.cos(angle), jnp.sin(angle)

    load_uq.wait()
    load_qr.wait()
    others = pl.ds(0, F - 1)
    rcopy(ps.at[others], pr.at[others], sp.at[0], rp.at[0], f, hd).wait_recv()
    probes = pr[...].astype(f32).reshape(queries, slice_rank).astype(bf16)

    def nope_of(p, j):
        return jnp.dot(probes, uq[:, block(p * U + j, cols)], preferred_element_type=f32)

    def rope_of(p):
        return jnp.dot(probes, wqr[:, block(p, brcols)], preferred_element_type=f32)

    beside = u * 4 + v * 2 + 1 - core
    along = u * 4 + (1 - v) * 2 + core

    def pair_copy(vv, j):
        return rcopy(pp.at[vv, j], pv.at[vv, j], spp.at[0], rpp.at[vv * U + j], beside, hd)

    def pair_rope(vv):
        return rcopy(ppr.at[vv], pvr.at[vv], sppr.at[0], rppr.at[vv], beside, hd)

    def line_copy(j):
        return rcopy(ls.at[j], lr.at[j], sl.at[0], rl.at[j], along, hd)

    def line_rope():
        return rcopy(lsr, lrr, slr.at[0], rlr.at[0], along, hd)

    def far(k):
        return lax.rem(u + k, U)

    def half_copy(j, k):
        return rcopy(hs.at[j], hr.at[u, j], sh.at[j], rh.at[j], far(k) * 4 + quad, hd)

    def half_rope(k):
        return rcopy(hsr.at[far(k)], hrr.at[u], shr.at[0], rhr.at[0], far(k) * 4 + quad, hd)

    for vv in (1 - v, v):
        for j in range(U):
            pp[vv, j] = nope_of((1 - core) * 2 + vv, j).astype(bf16)
            pair_copy(vv, j).start()
    for j in range(U):
        a = nope_of(core * 2 + 1 - v, j)
        pair_copy(1 - v, j).wait_recv()
        ls[j] = (a + pv[1 - v, j].astype(f32)).astype(bf16)
        line_copy(j).start()
    for vv in (1 - v, v):
        ppr[vv] = rope_of((1 - core) * 2 + vv).astype(bf16)
        pair_rope(vv).start()
    nope = []
    for j in range(U):
        a = nope_of(part, j)
        pair_copy(v, j).wait_recv()
        nope.append(a + pv[v, j].astype(f32))
    a = rope_of(core * 2 + 1 - v)
    pair_rope(1 - v).wait_recv()
    lsr[...] = (a + pvr[1 - v].astype(f32)).astype(bf16)
    line_rope().start()
    rope = rope_of(part)
    pair_rope(v).wait_recv()
    rope = rope + pvr[v].astype(f32)
    for j in range(U):
        line_copy(j).wait_recv()
        nope[j] = nope[j] + lr[j].astype(f32)
        hs[j] = nope[j].astype(bf16)
        each(1, U, functools.partial(half_copy, j), "start")
    line_rope().wait_recv()
    rope = rope + lrr[...].astype(f32)
    for uu in range(U):
        hsr[uu] = rope[uu * half_queries:(uu + 1) * half_queries].astype(bf16)
    each(1, U, half_rope, "start")
    each(1, 4, functools.partial(weight_copy, 1), "start")

    er = iota((expanded, queries), 0)
    ed = lax.div(er, per)
    es = lax.div(lax.rem(er, per), own)
    pick = (lax.div(ed, G) * (steps * G) + es * G + lax.rem(ed, G)) == iota((expanded, queries), 1)
    pick = jnp.where(pick, 1.0, 0.0).astype(bf16)
    head_of_row = lax.rem(iota((expanded, cols), 0), own)
    own_head = lax.div(iota((expanded, cols), 1), NOPE) == head_of_row

    load_uk.wait()
    weight_wait(0, "wait_recv")
    for j in range(U):
        got = hr.at[pl.ds(0, U - 1), j]
        rcopy(got, got, sh.at[j], rh.at[j], f, hd).wait_recv()
        total = nope[j]
        for k in range(1, U):
            total = total + hr[far(k), j].astype(f32)
        wide = jnp.where(own_head, jnp.dot(pick, total.astype(bf16), preferred_element_type=f32), 0.0).astype(bf16)
        latent = lax.dot_general(
            wide, wk[:, j * cols:(j + 1) * cols], (((1,), (1,)), ((), ())), preferred_element_type=f32
        )
        qs[:, j * per:(j + 1) * per, :] = latent.reshape(N, per, wide_c).astype(bf16)

    def tile(p, uu):
        return (pl.ds(pl.multiple_of(p * tall, 16), tall), pl.ds(pl.multiple_of(uu * wide_c, 128), wide_c))

    def spread(k):
        return lax.rem(u + 1 + lax.div(k, 4), U) * 4 + lax.rem(quad + lax.rem(k, 4), 4)

    def query_copy(hh, k):
        ff = spread(k)
        return rcopy(qs.at[ff * G + hh], qr.at[tile(hd * 4 + part, u)], sq.at[0], rq.at[hd], ff, hh)

    def own_column(k, carry):
        @pl.when(spread(k) != f)
        def _():
            query_copy(hd, k).start()
        return carry

    lax.fori_loop(0, F, own_column, 0)
    qr[tile(hd * 4 + part, u)] = qs[pl.ds(me, 1)].reshape(tall, wide_c)

    got = hrr.at[pl.ds(0, U - 1)]
    rcopy(got, got, shr.at[0], rhr.at[0], f, hd).wait_recv()
    turned = hsr[u].astype(f32)
    for k in range(1, U):
        turned = turned + hrr[far(k)].astype(f32)
    turned = turned.astype(bf16)
    near = N // U
    rows_r = near * tall
    rr = iota((rows_r, half_queries), 0)
    rd = lax.div(rr, tall)
    rs = lax.div(lax.rem(rr, per), own)
    pick_r = (lax.div(rd, G) * (steps * G) + rs * G + lax.rem(rd, G)) == iota((rows_r, half_queries), 1)
    pick_r = jnp.where(pick_r, 1.0, 0.0).astype(bf16)
    rh_row = lax.rem(iota((rows_r, brcols), 0), tall)
    rh_row = lax.div(rh_row, per) * own + lax.rem(rh_row, own)
    own_rope = lax.div(iota((rows_r, brcols), 1), R) == rh_row
    fold = lax.rem(iota((brcols, 128), 0), R) == iota((brcols, 128), 1)
    fold = jnp.where(fold, 1.0, 0.0).astype(bf16)
    wide_rope = jnp.where(own_rope, jnp.dot(pick_r, turned, preferred_element_type=f32), 0.0).astype(bf16)
    es_[...] = jnp.dot(wide_rope, fold, preferred_element_type=f32).reshape(near, tall, 128).astype(bf16)
    here_r = quad * G + hd

    def rope_copy(k):
        t = lax.rem(here_r + k, near)
        return rcopy(es_.at[t], er_.at[hd * 4 + part], se.at[0], re_.at[hd], u * 4 + lax.div(t, G), lax.rem(t, G))

    each(1, near, rope_copy, "start")
    er_[pl.ds(hd * 4 + part, 1)] = es_[pl.ds(here_r, 1)]

    def other_columns(k, carry):
        query_copy(lax.rem(hd + lax.div(k, F), G), lax.rem(k, F)).start()
        return carry

    lax.fori_loop(F, N, other_columns, 0)

    load_kv.wait()
    factor = (NOPE + R) ** -0.5
    chunk = F
    keys = stored + 128
    sr = iota((128, 128), 0)
    sc = iota((128, 128), 1)
    half = R // 2
    swap = jnp.where((sr == sc + half) & (sc < half), -1.0, 0.0)
    swap = swap + jnp.where((sr == sc - half) & (sc >= half) & (sc < R), 1.0, 0.0)
    swap = swap.astype(bf16)
    rows = chunk * per
    cosines = jnp.broadcast_to(cos8[None], (chunk, per, 128)).reshape(rows, 128)
    sines = jnp.broadcast_to(sin8[None], (chunk, per, 128)).reshape(rows, 128)
    column = iota((rows, keys), 1)
    step_of = lax.div(lax.rem(iota((rows, keys), 0), per), own)
    shown = (column < len_ref[0]) | ((column >= stored) & (column <= stored + step_of))

    def mixed_copy(b, i):
        p = lax.rem(i, 2) * 2 + lax.rem(lax.div(i, 2), 2)
        return rcopy(ms.at[tile(b * 4 + p, lax.div(i, 4))], mr.at[me], sm.at[0], rm.at[0], i, b)

    def attend_chunk(turn, carry):
        b = lax.rem(hd + G - turn, G)

        def arrived(n, m):
            q = qs.at[pl.ds(0, n)]
            rcopy(q, q, sq.at[0], rq.at[b], f, hd).wait_recv()
            e = es_.at[pl.ds(0, m)]
            rcopy(e, e, se.at[0], re_.at[b], f, hd).wait_recv()

        @pl.when(turn == 0)
        def _():
            arrived(F - 1, 3)

        @pl.when(turn > 0)
        def _():
            arrived(F, 4)

        here = pl.ds(pl.multiple_of(b * rows, 16), rows)
        lat = qr[here, :]
        xr = er_[pl.ds(b * 4, 4)].astype(f32).reshape(rows, 128)
        turned = jnp.dot(xr.astype(bf16), swap, preferred_element_type=f32)
        rot = (xr * cosines + turned * sines).astype(bf16)[:, 0:R]
        nt = (((1,), (1,)), ((), ()))
        s = jnp.dot(lat, kv[0:C, :], preferred_element_type=f32)
        s = s + jnp.dot(rot, kv[C:C + R, :], preferred_element_type=f32)
        n = lax.dot_general(lat, fresh[:, 0:C], nt, preferred_element_type=f32)
        n = n + lax.dot_general(rot, fresh[:, C:C + R], nt, preferred_element_type=f32)
        s = jnp.concatenate([s, n], axis=1)
        s = jnp.where(shown, s * factor, -1e30)
        m = jnp.max(s, axis=1, keepdims=True)
        w = jnp.exp(s - m)
        total = jnp.sum(w, axis=1, keepdims=True)
        w = w.astype(bf16)
        mix = lax.dot_general(w[:, 0:stored], kv[0:C, :], nt, preferred_element_type=f32)
        mix = mix + jnp.dot(w[:, stored:], fresh[:, 0:C], preferred_element_type=f32)
        ms[here, :] = (mix / total).astype(bf16)

        def send(k, c):
            i = spread(k)

            @pl.when(i * G + b != me)
            def _():
                mixed_copy(b, i).start()
            return c

        lax.fori_loop(0, chunk, send, 0)
        return carry

    lax.fori_loop(0, G, attend_chunk, 0)
    mr[pl.ds(me, 1)] = ms[tile(hd * 4 + part, u)].reshape(1, tall, wide_c)

    load_uv.wait()
    weight_wait(1, "wait_recv")
    most = mr.at[pl.ds(0, N - 1)]
    rcopy(most, most, sm.at[0], rm.at[0], f, hd).wait_recv()
    for j in range(U):
        mixed = mr[:, j * per:(j + 1) * per, :].astype(f32).reshape(expanded, wide_c).astype(bf16)
        values = jnp.dot(mixed, wv[:, j * cols:(j + 1) * cols], preferred_element_type=f32)
        values = jnp.where(own_head, values, 0.0).astype(bf16)
        values = lax.dot_general(pick, values, (((0,), (0,)), ((), ())), preferred_element_type=f32)
        vs[:, :, j * cols:(j + 1) * cols] = values.reshape(F, steps * G, cols).astype(bf16)

    def out_copy(k):
        t = spread(k)
        return rcopy(vs.at[t], vr.at[f], so.at[0], ro.at[0], t, hd)

    def out_send(k, carry):
        @pl.when(spread(k) != f)
        def _():
            out_copy(k).start()
        return carry

    lax.fori_loop(0, F, out_send, 0)
    vr[pl.ds(f, 1)] = vs[pl.ds(f, 1)]

    rcopy(vs.at[others], vr.at[others], so.at[0], ro.at[0], f, hd).wait_recv()
    for p in range(4):
        q = (p % 2) * 2 + p // 2
        a = sum(vr[uu * 4 + q].astype(f32) for uu in range(U))
        for s in range(steps):
            out_ref[s, :, p * bcols:(p + 1) * bcols] = a[s * G:(s + 1) * G].astype(bf16)

    rcopy(ps.at[others], pr.at[others], sp.at[0], rp.at[0], f, hd).wait_send()
    weight_wait(0, "wait_send")
    weight_wait(1, "wait_send")
    rcopy(pp, pv, spp.at[0], rpp.at[0], f, hd).wait_send()
    rcopy(ppr, pvr, sppr.at[0], rppr.at[0], f, hd).wait_send()
    rcopy(ls, lr, sl.at[0], rl.at[0], f, hd).wait_send()
    line_rope().wait_send()
    for j in range(U):
        each(1, U, functools.partial(half_copy, j), "wait_send")
    each(1, U, half_rope, "wait_send")
    sent = es_.at[pl.ds(0, near - 1)]
    rcopy(sent, sent, se.at[0], re_.at[0], f, hd).wait_send()
    sent = qs.at[pl.ds(0, N - 1)]
    rcopy(sent, sent, sq.at[0], rq.at[0], f, hd).wait_send()
    rcopy(most, most, sm.at[0], rm.at[0], f, hd).wait_send()
    rcopy(vs.at[others], vr.at[others], so.at[0], ro.at[0], f, hd).wait_send()


def one_kernel(probe_compressed, w_uq, w_qr, w_uk, w_uv, cache, new_kv, lengths):
    F, G = lax.axis_size("fsdp"), lax.axis_size("head")
    N, U = F * G, F // 4
    steps, group, _ = probe_compressed.shape
    ck, heads = w_uk.shape[0], w_uk.shape[1] // NOPE
    own = heads // F
    C = ck * F
    queries = F * steps * G
    per = steps * own
    tall = U * per
    cols, rcols = own * NOPE, own * R
    bcols, brcols = U * cols, U * rcols
    cache = cache.transpose(0, 2, 1)
    new_kv = new_kv.transpose(1, 0, 2)
    half = R // 2
    freqs = 10000.0 ** (-(np.arange(half, dtype=np.float32) * 2.0 / R))
    freqs = np.concatenate([freqs, freqs, np.zeros(128 - R)]).astype(np.float32)[None]
    bf16 = jnp.bfloat16
    vm = lambda *shape: pltpu.VMEM(shape, bf16)
    dma = lambda n: pltpu.SemaphoreType.DMA((n,))
    vmem = pl.BlockSpec(memory_space=pltpu.VMEM)
    hbm = pl.BlockSpec(memory_space=pltpu.HBM)
    return pl.pallas_call(
        functools.partial(fused, F, G, steps, own),
        out_shape=jax.ShapeDtypeStruct((steps, group, heads * VDIM), bf16),
        in_specs=[pl.BlockSpec(memory_space=pltpu.SMEM)] + [hbm] * 8,
        out_specs=vmem,
        scratch_shapes=[
            pltpu.VMEM((1, 128), jnp.float32), vm(*probe_compressed.shape), vm(*new_kv.shape),
            vm(*w_uq.shape), vm(*w_qr.shape), vm(4 * ck, bcols), vm(4 * ck, bcols), vm(*cache.shape[1:]),
            vm(F, steps * G, w_uq.shape[0]), vm(F, steps * G, w_uq.shape[0]),
            vm(2, U, queries, cols), vm(2, U, queries, cols),
            vm(2, queries, brcols), vm(2, queries, brcols),
            vm(U, queries, cols), vm(U, queries, cols), vm(queries, brcols), vm(queries, brcols),
            vm(U, queries, cols), vm(U, U, queries, cols),
            vm(U, queries // U, brcols), vm(U, queries // U, brcols),
            vm(N // U, tall, 128), vm(4 * G, tall, 128),
            vm(N, tall, 4 * ck), vm(4 * G * tall, C), vm(4 * G * tall, C), vm(N, tall, 4 * ck),
            vm(F, steps * G, bcols), vm(F, steps * G, bcols),
            dma(8), dma(1), dma(1), dma(2), dma(2), dma(1), dma(2 * U), dma(1), dma(2),
            dma(1), dma(U), dma(1), dma(1), dma(U), dma(U), dma(1), dma(1),
            dma(1), dma(G), dma(1), dma(G), dma(1), dma(1), dma(1), dma(1),
        ],
        compiler_params=pltpu.CompilerParams(
            collective_id=0, has_side_effects=True, vmem_limit_bytes=67043328
        ),
    )(lengths, jnp.asarray(freqs), probe_compressed, new_kv, w_uq, w_qr, w_uk, w_uv, cache)


def choose(*arrays):
    probe, w_uk, cache = arrays[0], arrays[3], arrays[5]
    F, G = lax.axis_size("fsdp"), lax.axis_size("head")
    own = w_uk.shape[1] // NOPE // F
    fits = own > 0 and w_uk.shape[1] == own * NOPE * F and F % 8 == 0
    fits = fits and probe.shape[1] == G and cache.shape[0] == 1
    fits = fits and (probe.shape[0] * own) % 8 == 0 and (probe.shape[0] * G) % 8 == 0
    fits = fits and w_uk.shape[0] % 16 == 0 and (4 * w_uk.shape[0]) % 128 == 0 and cache.shape[1] % 128 == 0 and (own * R) % 128 == 0
    return one_kernel(*arrays) if fits else per_device(*arrays)


def solution(mesh):
    in_specs = (
        P(None, "fsdp", None),
        P("fsdp", "head"),
        P("fsdp", "head"),
        P("fsdp", "head"),
        P("fsdp", "head"),
        P(("fsdp", "head"), None, None),
        P(None, ("fsdp", "head"), None),
        P(("fsdp", "head")),
    )
    out_specs = P(None, "fsdp", "head")
    return jax.shard_map(
        choose, mesh=mesh, in_specs=in_specs, out_specs=out_specs, check_vma=False
    )
```

time: 58.1 us -> 50.5 us (0.87)
  Pallas kernels: 55.7 us -> 47.9 us
    pallas_call x1, Pallas kernels: 55.7 us -> 47.9 us  [one_kernel(): pl.pallas_call(functools.partial(fused, F, G, steps, own), out_shape=jax....]
where the time goes in v1:
time: 50.5 us; the launch traced here: 50 us
  Pallas kernels  47.9 us (95%)
  local copies, waits for them, and re-layouts  1.49 us (3%)
  between operations  0.66 us (1%)
    pallas_call x1, Pallas kernels, one_kernel(): pl.pallas_call(functools.partial(fused, F, G, steps, own), out_shape=jax....  47.9 us
    unnamed x1, local copies, waits for them, and re-layouts  1.49 us

profile of v1, /device:TPU:1, one launch (start us, length us, event | category | flops | bytes accessed | tf_op | source)
XLA Modules:
  0.0 50.0 jit_solution(17202930565206837363)
XLA Ops:
  0.7 47.9 %shard_map.91 = bf16[2,4,4096]{2,1,0:T(4,128)(2,1)} custom-call(s32[1]{0:T(128)S(6)} %copy.11.len_ref, f32[1,128]{1,0:T(1,128)} %constant.2.clone.freq_hbm, bf16[2,4,1536]{2,1,0:T(4,128)(2,1)} %probe_hbm.1, bf16[1,2,576]{2,1,0:T(2,128)(2,1)} %bitcast.3, bf16[192,4096]{1,0:T(8,128)(2,1)} %uq_hbm.1, bf16[192,2048]{1,0:T(8,128)(2,1)} %qr_hbm.1, ...), custom_call_target="tpu_custom_call" | custom-call | tf_op jit(solution)/shard_map/pallas_call | solution.py:496
  48.5 1.5 %copy.12 = bf16[2,4,4096]{2,1,0:T(4,128)(2,1)} copy(bf16[2,4,4096]{2,1,0:T(4,128)(2,1)} %shard_map.91) | data formatting | bytes 131072

commit v2 on v1

--- a/solution.py
+++ b/solution.py
@@ -144,12 +144,18 @@
     load_uq = pltpu.make_async_copy(uq_hbm, uq, lsem.at[0])
     load_qr = pltpu.make_async_copy(qr_hbm, wqr, lsem.at[1])
     load_kv = pltpu.make_async_copy(cache_hbm.at[0], kv, lsem.at[2])
-    load_uk = pltpu.make_async_copy(uk_hbm.at[:, block(part, bcols)], wk.at[mine], lsem.at[3])
-    load_uv = pltpu.make_async_copy(uv_hbm.at[:, block(part, bcols)], wv.at[mine], lsem.at[4])
-    load_probe = pltpu.make_async_copy(probe_hbm, probe_ref, lsem.at[5])
-    load_new = pltpu.make_async_copy(new_hbm, new_ref, lsem.at[6])
-    load_freq = pltpu.make_async_copy(freq_hbm, freq_ref, lsem.at[7])
-    loads = [load_probe, load_uq, load_qr, load_new, load_freq, load_uk, load_kv, load_uv]
+    load_uk = [
+        pltpu.make_async_copy(uk_hbm.at[:, block(part * U + j, cols)], wk.at[j, mine], lsem.at[7 + j])
+        for j in range(U)
+    ]
+    load_uv = [
+        pltpu.make_async_copy(uv_hbm.at[:, block(part * U + j, cols)], wv.at[j, mine], lsem.at[7 + U + j])
+        for j in range(U)
+    ]
+    load_probe = pltpu.make_async_copy(probe_hbm, probe_ref, lsem.at[3])
+    load_new = pltpu.make_async_copy(new_hbm, new_ref, lsem.at[4])
+    load_freq = pltpu.make_async_copy(freq_hbm, freq_ref, lsem.at[5])
+    loads = [load_probe, load_uq, load_qr, load_new, load_freq, *load_uk, load_kv, *load_uv]
     for c in loads:
         c.start()
 
@@ -177,18 +183,22 @@
         t = lax.rem(f + k, F)
         return rcopy(ps.at[t], pr.at[f], sp.at[0], rp.at[0], t, hd)
 
-    def weight_copy(i, k):
+    def weight_copy(i, j, k):
         hbm, w = ((uk_hbm, wk), (uv_hbm, wv))[i]
-        t = lax.rem(quad + k, 4)
+        t = lax.rem(v + k // 2, 2) * 2 + lax.rem(core + k, 2)
         there = lax.rem(t, 2) * 2 + lax.div(t, 2)
-        return rcopy(hbm.at[:, block(there, bcols)], w.at[mine], sk.at[i], rk.at[i], u * 4 + t, hd)
-
-    def weight_wait(i, method):
-        w = (wk, wv)[i].at[pl.ds(0, 3 * ck)]
-        getattr(rcopy(w, w, sk.at[i], rk.at[i], f, hd), method)()
+        return rcopy(hbm.at[:, block(there * U + j, cols)], w.at[j, mine], sk.at[i, j], rk.at[i, j], u * 4 + t, hd)
+
+    def weight_wait(i, j, method):
+        w = (wk, wv)[i].at[j, pl.ds(0, 3 * ck)]
+        getattr(rcopy(w, w, sk.at[i, j], rk.at[i, j], f, hd), method)()
 
     each(1, F, probe_copy, "start")
-    each(1, 4, functools.partial(weight_copy, 0), "start")
+    weight_copy(0, 0, 1).start()
+    weight_copy(0, 0, 2).start()
+    weight_copy(0, 0, 3).start()
+    weight_copy(0, 1, 1).start()
+    weight_copy(0, 1, 2).start()
 
     load_new.wait()
     load_freq.wait()
@@ -238,41 +248,61 @@
     def half_rope(k):
         return rcopy(hsr.at[far(k)], hrr.at[u], shr.at[0], rhr.at[0], far(k) * 4 + quad, hd)
 
-    for vv in (1 - v, v):
-        for j in range(U):
-            pp[vv, j] = nope_of((1 - core) * 2 + vv, j).astype(bf16)
-            pair_copy(vv, j).start()
-    for j in range(U):
+    def pair_nope(vv, j):
+        pp[vv, j] = nope_of((1 - core) * 2 + vv, j).astype(bf16)
+        pair_copy(vv, j).start()
+
+    def pair_turn(vv):
+        ppr[vv] = rope_of((1 - core) * 2 + vv).astype(bf16)
+        pair_rope(vv).start()
+
+    def line_nope(j):
         a = nope_of(core * 2 + 1 - v, j)
         pair_copy(1 - v, j).wait_recv()
         ls[j] = (a + pv[1 - v, j].astype(f32)).astype(bf16)
         line_copy(j).start()
-    for vv in (1 - v, v):
-        ppr[vv] = rope_of((1 - core) * 2 + vv).astype(bf16)
-        pair_rope(vv).start()
-    nope = []
-    for j in range(U):
-        a = nope_of(part, j)
-        pair_copy(v, j).wait_recv()
-        nope.append(a + pv[v, j].astype(f32))
+
+    pair_nope(1 - v, 0)
+    pair_turn(1 - v)
+    for j in range(1, U):
+        pair_nope(1 - v, j)
+    pair_nope(v, 0)
+    line_nope(0)
     a = rope_of(core * 2 + 1 - v)
     pair_rope(1 - v).wait_recv()
     lsr[...] = (a + pvr[1 - v].astype(f32)).astype(bf16)
     line_rope().start()
+    for j in range(1, U):
+        line_nope(j)
+    weight_copy(0, 1, 3).start()
+    pair_turn(v)
+    for j in range(1, U):
+        pair_nope(v, j)
+    nope = [nope_of(part, j) for j in range(U)]
     rope = rope_of(part)
+    for j in range(U):
+        pair_copy(v, j).wait_recv()
+        nope[j] = nope[j] + pv[v, j].astype(f32)
     pair_rope(v).wait_recv()
     rope = rope + pvr[v].astype(f32)
-    for j in range(U):
+
+    def half_nope(j):
         line_copy(j).wait_recv()
         nope[j] = nope[j] + lr[j].astype(f32)
         hs[j] = nope[j].astype(bf16)
         each(1, U, functools.partial(half_copy, j), "start")
+
+    half_nope(0)
     line_rope().wait_recv()
     rope = rope + lrr[...].astype(f32)
     for uu in range(U):
         hsr[uu] = rope[uu * half_queries:(uu + 1) * half_queries].astype(bf16)
     each(1, U, half_rope, "start")
-    each(1, 4, functools.partial(weight_copy, 1), "start")
+    for j in range(1, U):
+        half_nope(j)
+    weight_copy(1, 0, 1).start()
+    weight_copy(1, 0, 2).start()
+    weight_copy(1, 0, 3).start()
 
     er = iota((expanded, queries), 0)
     ed = lax.div(er, per)
@@ -282,77 +312,77 @@
     head_of_row = lax.rem(iota((expanded, cols), 0), own)
     own_head = lax.div(iota((expanded, cols), 1), NOPE) == head_of_row
 
-    load_uk.wait()
-    weight_wait(0, "wait_recv")
-    for j in range(U):
+    spread = [lax.rem(u + 1 + k // 4, U) * 4 + lax.rem(quad + k % 4, 4) for k in range(F)]
+    columns = [lax.rem(hd + k, G) for k in range(G)]
+    others_of = [(ff, hh) for ff in spread for hh in columns if ff is not spread[-4] or hh is not columns[0]]
+
+    def rows_of(p):
+        return pl.ds(pl.multiple_of(p * per, 8), per)
+
+    def c_of(uu):
+        return pl.ds(pl.multiple_of(uu * wide_c, 128), wide_c)
+
+    def to_all(copy):
+        for ff, hh in others_of:
+            copy(ff, hh).start()
+
+    def query_copy(j, ff, hh):
+        return rcopy(
+            qs.at[j, ff * G + hh], qr.at[j, rows_of(hd * 4 + part), c_of(u)], sq.at[j], rq.at[j], ff, hh
+        )
+
+    near = N // U
+
+    def dispatch_rope():
+        got = hrr.at[pl.ds(0, U - 1)]
+        rcopy(got, got, shr.at[0], rhr.at[0], f, hd).wait_recv()
+        turned = hsr[u].astype(f32)
+        for k in range(1, U):
+            turned = turned + hrr[far(k)].astype(f32)
+        turned = turned.astype(bf16)
+        rows_r = near * tall
+        rr = iota((rows_r, half_queries), 0)
+        rd = lax.div(rr, tall)
+        rs = lax.div(lax.rem(rr, per), own)
+        pick_r = (lax.div(rd, G) * (steps * G) + rs * G + lax.rem(rd, G)) == iota((rows_r, half_queries), 1)
+        pick_r = jnp.where(pick_r, 1.0, 0.0).astype(bf16)
+        rh_row = lax.rem(iota((rows_r, brcols), 0), tall)
+        rh_row = lax.div(rh_row, per) * own + lax.rem(rh_row, own)
+        own_rope = lax.div(iota((rows_r, brcols), 1), R) == rh_row
+        fold = lax.rem(iota((brcols, 128), 0), R) == iota((brcols, 128), 1)
+        fold = jnp.where(fold, 1.0, 0.0).astype(bf16)
+        wide_rope = jnp.where(own_rope, jnp.dot(pick_r, turned, preferred_element_type=f32), 0.0).astype(bf16)
+        es_[...] = jnp.dot(wide_rope, fold, preferred_element_type=f32).reshape(near, tall, 128).astype(bf16)
+        here_r = quad * G + hd
+
+        def rope_copy(k):
+            t = lax.rem(here_r + k, near)
+            return rcopy(es_.at[t], er_.at[hd * 4 + part], se.at[0], re_.at[0], u * 4 + lax.div(t, G), lax.rem(t, G))
+
+        each(1, near, rope_copy, "start")
+        er_[pl.ds(hd * 4 + part, 1)] = es_[pl.ds(here_r, 1)]
+
+    for j in range(U):
+        load_uk[j].wait()
+        weight_wait(0, j, "wait_recv")
         got = hr.at[pl.ds(0, U - 1), j]
         rcopy(got, got, sh.at[j], rh.at[j], f, hd).wait_recv()
         total = nope[j]
         for k in range(1, U):
             total = total + hr[far(k), j].astype(f32)
         wide = jnp.where(own_head, jnp.dot(pick, total.astype(bf16), preferred_element_type=f32), 0.0).astype(bf16)
-        latent = lax.dot_general(
-            wide, wk[:, j * cols:(j + 1) * cols], (((1,), (1,)), ((), ())), preferred_element_type=f32
-        )
-        qs[:, j * per:(j + 1) * per, :] = latent.reshape(N, per, wide_c).astype(bf16)
-
-    def tile(p, uu):
-        return (pl.ds(pl.multiple_of(p * tall, 16), tall), pl.ds(pl.multiple_of(uu * wide_c, 128), wide_c))
-
-    def spread(k):
-        return lax.rem(u + 1 + lax.div(k, 4), U) * 4 + lax.rem(quad + lax.rem(k, 4), 4)
-
-    def query_copy(hh, k):
-        ff = spread(k)
-        return rcopy(qs.at[ff * G + hh], qr.at[tile(hd * 4 + part, u)], sq.at[0], rq.at[hd], ff, hh)
-
-    def own_column(k, carry):
-        @pl.when(spread(k) != f)
-        def _():
-            query_copy(hd, k).start()
-        return carry
-
-    lax.fori_loop(0, F, own_column, 0)
-    qr[tile(hd * 4 + part, u)] = qs[pl.ds(me, 1)].reshape(tall, wide_c)
-
-    got = hrr.at[pl.ds(0, U - 1)]
-    rcopy(got, got, shr.at[0], rhr.at[0], f, hd).wait_recv()
-    turned = hsr[u].astype(f32)
-    for k in range(1, U):
-        turned = turned + hrr[far(k)].astype(f32)
-    turned = turned.astype(bf16)
-    near = N // U
-    rows_r = near * tall
-    rr = iota((rows_r, half_queries), 0)
-    rd = lax.div(rr, tall)
-    rs = lax.div(lax.rem(rr, per), own)
-    pick_r = (lax.div(rd, G) * (steps * G) + rs * G + lax.rem(rd, G)) == iota((rows_r, half_queries), 1)
-    pick_r = jnp.where(pick_r, 1.0, 0.0).astype(bf16)
-    rh_row = lax.rem(iota((rows_r, brcols), 0), tall)
-    rh_row = lax.div(rh_row, per) * own + lax.rem(rh_row, own)
-    own_rope = lax.div(iota((rows_r, brcols), 1), R) == rh_row
-    fold = lax.rem(iota((brcols, 128), 0), R) == iota((brcols, 128), 1)
-    fold = jnp.where(fold, 1.0, 0.0).astype(bf16)
-    wide_rope = jnp.where(own_rope, jnp.dot(pick_r, turned, preferred_element_type=f32), 0.0).astype(bf16)
-    es_[...] = jnp.dot(wide_rope, fold, preferred_element_type=f32).reshape(near, tall, 128).astype(bf16)
-    here_r = quad * G + hd
-
-    def rope_copy(k):
-        t = lax.rem(here_r + k, near)
-        return rcopy(es_.at[t], er_.at[hd * 4 + part], se.at[0], re_.at[hd], u * 4 + lax.div(t, G), lax.rem(t, G))
-
-    each(1, near, rope_copy, "start")
-    er_[pl.ds(hd * 4 + part, 1)] = es_[pl.ds(here_r, 1)]
-
-    def other_columns(k, carry):
-        query_copy(lax.rem(hd + lax.div(k, F), G), lax.rem(k, F)).start()
-        return carry
-
-    lax.fori_loop(F, N, other_columns, 0)
+        latent = lax.dot_general(wide, wk[j], (((1,), (1,)), ((), ())), preferred_element_type=f32)
+        qs[j] = latent.reshape(N, per, wide_c).astype(bf16)
+        to_all(functools.partial(query_copy, j))
+        qr[j, rows_of(hd * 4 + part), c_of(u)] = qs[j, pl.ds(me, 1)].reshape(per, wide_c)
+        if j == 0:
+            dispatch_rope()
+    weight_copy(1, 1, 1).start()
+    weight_copy(1, 1, 2).start()
+    weight_copy(1, 1, 3).start()
 
     load_kv.wait()
     factor = (NOPE + R) ** -0.5
-    chunk = F
     keys = stored + 128
     sr = iota((128, 128), 0)
     sc = iota((128, 128), 1)
@@ -360,40 +390,28 @@
     swap = jnp.where((sr == sc + half) & (sc < half), -1.0, 0.0)
     swap = swap + jnp.where((sr == sc - half) & (sc >= half) & (sc < R), 1.0, 0.0)
     swap = swap.astype(bf16)
-    rows = chunk * per
-    cosines = jnp.broadcast_to(cos8[None], (chunk, per, 128)).reshape(rows, 128)
-    sines = jnp.broadcast_to(sin8[None], (chunk, per, 128)).reshape(rows, 128)
+    rows = 4 * G * per
+    cosines = jnp.broadcast_to(cos8[None], (4 * G, per, 128)).reshape(rows, 128)
+    sines = jnp.broadcast_to(sin8[None], (4 * G, per, 128)).reshape(rows, 128)
     column = iota((rows, keys), 1)
     step_of = lax.div(lax.rem(iota((rows, keys), 0), per), own)
     shown = (column < len_ref[0]) | ((column >= stored) & (column <= stored + step_of))
-
-    def mixed_copy(b, i):
-        p = lax.rem(i, 2) * 2 + lax.rem(lax.div(i, 2), 2)
-        return rcopy(ms.at[tile(b * 4 + p, lax.div(i, 4))], mr.at[me], sm.at[0], rm.at[0], i, b)
-
-    def attend_chunk(turn, carry):
-        b = lax.rem(hd + G - turn, G)
-
-        def arrived(n, m):
-            q = qs.at[pl.ds(0, n)]
-            rcopy(q, q, sq.at[0], rq.at[b], f, hd).wait_recv()
-            e = es_.at[pl.ds(0, m)]
-            rcopy(e, e, se.at[0], re_.at[b], f, hd).wait_recv()
-
-        @pl.when(turn == 0)
-        def _():
-            arrived(F - 1, 3)
-
-        @pl.when(turn > 0)
-        def _():
-            arrived(F, 4)
-
-        here = pl.ds(pl.multiple_of(b * rows, 16), rows)
-        lat = qr[here, :]
-        xr = er_[pl.ds(b * 4, 4)].astype(f32).reshape(rows, 128)
+    nt = (((1,), (1,)), ((), ()))
+
+    def mixed_copy(j, ff, hh):
+        p = hh * 4 + lax.rem(ff, 2) * 2 + lax.rem(lax.div(ff, 2), 2)
+        return rcopy(ms.at[j, rows_of(p), c_of(lax.div(ff, 4))], mr.at[j, me], sm.at[j], rm.at[j], ff, hh)
+
+    for j in range(U):
+        got = qs.at[j, pl.ds(0, N - 1)]
+        rcopy(got, got, sq.at[j], rq.at[j], f, hd).wait_recv()
+        if j == 0:
+            got = es_.at[pl.ds(0, near - 1)]
+            rcopy(got, got, se.at[0], re_.at[0], f, hd).wait_recv()
+        lat = qr[j]
+        xr = er_[:, j * per:(j + 1) * per, :].astype(f32).reshape(rows, 128)
         turned = jnp.dot(xr.astype(bf16), swap, preferred_element_type=f32)
         rot = (xr * cosines + turned * sines).astype(bf16)[:, 0:R]
-        nt = (((1,), (1,)), ((), ()))
         s = jnp.dot(lat, kv[0:C, :], preferred_element_type=f32)
         s = s + jnp.dot(rot, kv[C:C + R, :], preferred_element_type=f32)
         n = lax.dot_general(lat, fresh[:, 0:C], nt, preferred_element_type=f32)
@@ -406,56 +424,41 @@
         w = w.astype(bf16)
         mix = lax.dot_general(w[:, 0:stored], kv[0:C, :], nt, preferred_element_type=f32)
         mix = mix + jnp.dot(w[:, stored:], fresh[:, 0:C], preferred_element_type=f32)
-        ms[here, :] = (mix / total).astype(bf16)
-
-        def send(k, c):
-            i = spread(k)
-
-            @pl.when(i * G + b != me)
-            def _():
-                mixed_copy(b, i).start()
-            return c
-
-        lax.fori_loop(0, chunk, send, 0)
-        return carry
-
-    lax.fori_loop(0, G, attend_chunk, 0)
-    mr[pl.ds(me, 1)] = ms[tile(hd * 4 + part, u)].reshape(1, tall, wide_c)
-
-    load_uv.wait()
-    weight_wait(1, "wait_recv")
-    most = mr.at[pl.ds(0, N - 1)]
-    rcopy(most, most, sm.at[0], rm.at[0], f, hd).wait_recv()
-    for j in range(U):
-        mixed = mr[:, j * per:(j + 1) * per, :].astype(f32).reshape(expanded, wide_c).astype(bf16)
-        values = jnp.dot(mixed, wv[:, j * cols:(j + 1) * cols], preferred_element_type=f32)
+        ms[j] = (mix / total).astype(bf16)
+        to_all(functools.partial(mixed_copy, j))
+        mr[j, pl.ds(me, 1)] = ms[j, rows_of(hd * 4 + part), c_of(u)].reshape(1, per, wide_c)
+
+    def out_copy(j, t):
+        return rcopy(vs.at[j, t], vr.at[j, f], so.at[j], ro.at[j], t, hd)
+
+    for j in range(U):
+        load_uv[j].wait()
+        weight_wait(1, j, "wait_recv")
+        most = mr.at[j, pl.ds(0, N - 1)]
+        rcopy(most, most, sm.at[j], rm.at[j], f, hd).wait_recv()
+        mixed = mr[j].astype(f32).reshape(expanded, wide_c).astype(bf16)
+        values = jnp.dot(mixed, wv[j], preferred_element_type=f32)
         values = jnp.where(own_head, values, 0.0).astype(bf16)
         values = lax.dot_general(pick, values, (((0,), (0,)), ((), ())), preferred_element_type=f32)
-        vs[:, :, j * cols:(j + 1) * cols] = values.reshape(F, steps * G, cols).astype(bf16)
-
-    def out_copy(k):
-        t = spread(k)
-        return rcopy(vs.at[t], vr.at[f], so.at[0], ro.at[0], t, hd)
-
-    def out_send(k, carry):
-        @pl.when(spread(k) != f)
-        def _():
-            out_copy(k).start()
-        return carry
-
-    lax.fori_loop(0, F, out_send, 0)
-    vr[pl.ds(f, 1)] = vs[pl.ds(f, 1)]
-
-    rcopy(vs.at[others], vr.at[others], so.at[0], ro.at[0], f, hd).wait_recv()
-    for p in range(4):
-        q = (p % 2) * 2 + p // 2
-        a = sum(vr[uu * 4 + q].astype(f32) for uu in range(U))
-        for s in range(steps):
-            out_ref[s, :, p * bcols:(p + 1) * bcols] = a[s * G:(s + 1) * G].astype(bf16)
+        vs[j] = values.reshape(F, steps * G, cols).astype(bf16)
+
+        for t in spread[:-4] + spread[-3:]:
+            out_copy(j, t).start()
+        vr[j, pl.ds(f, 1)] = vs[j, pl.ds(f, 1)]
+
+    for j in range(U):
+        got = vs.at[j, others]
+        rcopy(got, got, so.at[j], ro.at[j], f, hd).wait_recv()
+        for p in range(4):
+            q = (p % 2) * 2 + p // 2
+            a = sum(vr[j, uu * 4 + q].astype(f32) for uu in range(U))
+            for s in range(steps):
+                out_ref[s, :, (p * U + j) * cols:(p * U + j + 1) * cols] = a[s * G:(s + 1) * G].astype(bf16)
 
     rcopy(ps.at[others], pr.at[others], sp.at[0], rp.at[0], f, hd).wait_send()
-    weight_wait(0, "wait_send")
-    weight_wait(1, "wait_send")
+    for j in range(U):
+        weight_wait(0, j, "wait_send")
+        weight_wait(1, j, "wait_send")
     rcopy(pp, pv, spp.at[0], rpp.at[0], f, hd).wait_send()
     rcopy(ppr, pvr, sppr.at[0], rppr.at[0], f, hd).wait_send()
     rcopy(ls, lr, sl.at[0], rl.at[0], f, hd).wait_send()
@@ -465,10 +468,15 @@
     each(1, U, half_rope, "wait_send")
     sent = es_.at[pl.ds(0, near - 1)]
     rcopy(sent, sent, se.at[0], re_.at[0], f, hd).wait_send()
-    sent = qs.at[pl.ds(0, N - 1)]
-    rcopy(sent, sent, sq.at[0], rq.at[0], f, hd).wait_send()
-    rcopy(most, most, sm.at[0], rm.at[0], f, hd).wait_send()
-    rcopy(vs.at[others], vr.at[others], so.at[0], ro.at[0], f, hd).wait_send()
+    for j in range(U):
+        if True:
+            sent = qs.at[j, pl.ds(0, N - 1)]
+            rcopy(sent, sent, sq.at[j], rq.at[j], f, hd).wait_send()
+        if True:
+            sent = mr.at[j, pl.ds(0, N - 1)]
+            rcopy(sent, sent, sm.at[j], rm.at[j], f, hd).wait_send()
+        sent = vs.at[j, others]
+        rcopy(sent, sent, so.at[j], ro.at[j], f, hd).wait_send()
 
 
 def one_kernel(probe_compressed, w_uq, w_qr, w_uk, w_uv, cache, new_kv, lengths):
@@ -490,7 +498,7 @@
     freqs = np.concatenate([freqs, freqs, np.zeros(128 - R)]).astype(np.float32)[None]
     bf16 = jnp.bfloat16
     vm = lambda *shape: pltpu.VMEM(shape, bf16)
-    dma = lambda n: pltpu.SemaphoreType.DMA((n,))
+    dma = lambda *n: pltpu.SemaphoreType.DMA(n)
     vmem = pl.BlockSpec(memory_space=pltpu.VMEM)
     hbm = pl.BlockSpec(memory_space=pltpu.HBM)
     return pl.pallas_call(
@@ -500,7 +508,7 @@
         out_specs=vmem,
         scratch_shapes=[
             pltpu.VMEM((1, 128), jnp.float32), vm(*probe_compressed.shape), vm(*new_kv.shape),
-            vm(*w_uq.shape), vm(*w_qr.shape), vm(4 * ck, bcols), vm(4 * ck, bcols), vm(*cache.shape[1:]),
+            vm(*w_uq.shape), vm(*w_qr.shape), vm(U, 4 * ck, cols), vm(U, 4 * ck, cols), vm(*cache.shape[1:]),
             vm(F, steps * G, w_uq.shape[0]), vm(F, steps * G, w_uq.shape[0]),
             vm(2, U, queries, cols), vm(2, U, queries, cols),
             vm(2, queries, brcols), vm(2, queries, brcols),
@@ -508,11 +516,11 @@
             vm(U, queries, cols), vm(U, U, queries, cols),
             vm(U, queries // U, brcols), vm(U, queries // U, brcols),
             vm(N // U, tall, 128), vm(4 * G, tall, 128),
-            vm(N, tall, 4 * ck), vm(4 * G * tall, C), vm(4 * G * tall, C), vm(N, tall, 4 * ck),
-            vm(F, steps * G, bcols), vm(F, steps * G, bcols),
-            dma(8), dma(1), dma(1), dma(2), dma(2), dma(1), dma(2 * U), dma(1), dma(2),
+            vm(U, N, per, 4 * ck), vm(U, 4 * G * per, C), vm(U, 4 * G * per, C), vm(U, N, per, 4 * ck),
+            vm(U, F, steps * G, cols), vm(U, F, steps * G, cols),
+            dma(7 + 2 * U), dma(1), dma(1), dma(2, U), dma(2, U), dma(1), dma(2 * U), dma(1), dma(2),
             dma(1), dma(U), dma(1), dma(1), dma(U), dma(U), dma(1), dma(1),
-            dma(1), dma(G), dma(1), dma(G), dma(1), dma(1), dma(1), dma(1),
+            dma(1), dma(1), dma(U), dma(U), dma(U), dma(U), dma(U), dma(U),
         ],
         compiler_params=pltpu.CompilerParams(
             collective_id=0, has_side_effects=True, vmem_limit_bytes=67043328

time: 50.5 us -> 47.1 us (0.933)
  Pallas kernels: 47.9 us -> 44.4 us
    pallas_call x1, Pallas kernels: 47.9 us -> 44.4 us  [one_kernel(): pl.pallas_call(functools.partial(fused, F, G, steps, own), out_shape=jax....]
where the time goes in v2:
time: 47.1 us; the launch traced here: 46.5 us
  Pallas kernels  44.4 us (94%)
  local copies, waits for them, and re-layouts  1.49 us (3%)
  between operations  0.66 us (1%)
    pallas_call x1, Pallas kernels, one_kernel(): pl.pallas_call(functools.partial(fused, F, G, steps, own), out_shape=jax....  44.4 us
    unnamed x1, local copies, waits for them, and re-layouts  1.49 us

profile of v2, /device:TPU:1, one launch (start us, length us, event | category | flops | bytes accessed | tf_op | source)
XLA Modules:
  0.0 46.5 jit_solution(14895725026804393713)
XLA Ops:
  0.7 44.4 %shard_map.91 = bf16[2,4,4096]{2,1,0:T(4,128)(2,1)} custom-call(s32[1]{0:T(128)S(6)} %copy.11.len_ref, f32[1,128]{1,0:T(1,128)} %constant.2.clone.freq_hbm, bf16[2,4,1536]{2,1,0:T(4,128)(2,1)} %probe_hbm.1, bf16[1,2,576]{2,1,0:T(2,128)(2,1)} %bitcast.3, bf16[192,4096]{1,0:T(8,128)(2,1)} %uq_hbm.1, bf16[192,2048]{1,0:T(8,128)(2,1)} %qr_hbm.1, ...), custom_call_target="tpu_custom_call" | custom-call | tf_op jit(solution)/shard_map/pallas_call | solution.py:504
  45.0 1.5 %copy.12 = bf16[2,4,4096]{2,1,0:T(4,128)(2,1)} copy(bf16[2,4,4096]{2,1,0:T(4,128)(2,1)} %shard_map.91) | data formatting | bytes 131072
